TPU v7x, 32 devices: a whole 2x2x4 slice. The times are simulated.
32 devices in a mesh: seq: 16 (over z, x, core), row: 2 (over y).
Axes of the slice: x: 2, y: 2, z: 4, core: 2. Of those that a mesh axis runs over, the one named last changes fastest.
Arguments:
- patch_queries: bfloat16 [2048, 2048], P('seq', 'row'), may hold values from -15 to 15
- patch_keys: bfloat16 [2048, 2048], P('seq', 'row'), may hold values from -15 to 15
- patch_values: bfloat16 [2048, 2048], P('seq', 'row'), may hold values from -6 to 6
- patch_tasks: int32 [2048], P('seq'), may hold values from 0 to 7
- residual: bfloat16 [2048, 2048], P('seq', 'row'), may hold values from -6 to 6
- output_weight: bfloat16 [2048, 2048], P('row'), may hold values from -0.5 to 0.5
- global_down: bfloat16 [2048, 16], P('row'), may hold values from -0.5 to 0.5
- global_up: bfloat16 [16, 2048], P(None, 'row'), may hold values from -1.5 to 1.5
- global_scales: float32 [8, 16], replicated, may hold values from 0.25 to 4
- local_weight: bfloat16 [2048, 512], P('row'), may hold values from -0.125 to 0.125
- byte_ids: int32 [16384], P('seq'), may hold values from 0 to 255
- byte_table: bfloat16 [256, 512], replicated, may hold values from -6 to 6
- position_table: bfloat16 [8, 512], replicated, may hold values from -6 to 6
- norm_gain: float32 [512], replicated, may hold values from 0.5 to 1.5
- hidden_in: bfloat16 [2048, 512], P('row', 'seq'), may hold values from -0.25 to 0.25
- hidden_out: bfloat16 [2048, 512], P('row', 'seq'), may hold values from -0.125 to 0.125
- local_down: bfloat16 [512, 16], replicated, may hold values from -0.25 to 0.25
- local_up: bfloat16 [16, 2048], P(None, 'row'), may hold values from -1.5 to 1.5
- local_scales: float32 [8, 16], replicated, may hold values from 0.25 to 4
- cotangent: bfloat16 [16384, 512], P(('seq', 'row')), may hold values from -6 to 6
Outputs:
- grad_global_down: float32 [2048, 16], P('row')
- grad_global_up: float32 [16, 2048], P(None, 'row')
- grad_global_scales: float32 [8, 16], replicated
- grad_local_down: float32 [512, 16], replicated
- grad_local_up: float32 [16, 2048], P(None, 'row')
- grad_local_scales: float32 [8, 16], replicated
All inputs are finite; a program needn't handle non-finite values.
Results may differ from a plain program's by a relative error of at most 0.028.
Values may be sent and summed in bfloat16 or wider, within the bound.
A program may use at most 64 MiB of HBM per device.

v0:
```python
import math
import jax
import jax.numpy as jnp
from jax import lax
from jax.sharding import PartitionSpec as P

HEAD = 128
VOCAB = 256
PATCH = 8
TASKS = 8


def contract(left, right, left_dim, right_dim):
    return lax.dot_general(
        left, right, (((left_dim,), (right_dim,)), ((), ())), preferred_element_type=jnp.float32
    )


def select_rows(table, tasks):
    picks = (tasks[:, None] == jnp.arange(table.shape[0], dtype=jnp.int32)[None, :]).astype(
        jnp.float32
    )
    return jnp.dot(picks, table, precision=lax.Precision.HIGHEST)


def task_totals(tasks, values):
    picks = (tasks[:, None] == jnp.arange(TASKS, dtype=jnp.int32)[None, :]).astype(jnp.float32)
    return lax.dot_general(picks, values, (((0,), (0,)), ((), ())), precision=lax.Precision.HIGHEST)


def gelu_slope(upper):
    cumulative = 0.5 * (1.0 + lax.erf(upper * 0.7071067811865476))
    density = jnp.exp(-0.5 * upper * upper) * 0.3989422804014327
    return cumulative + upper * density


def local_inputs(
    identities, projected, tasks, byte_table, position_table, norm_gain, local_down, local_scales
):
    count = identities.shape[0]
    picks = (identities[:, None] == jnp.arange(VOCAB, dtype=jnp.int32)[None, :]).astype(
        jnp.bfloat16
    )
    embedded = jnp.dot(picks, byte_table, preferred_element_type=jnp.float32)
    patches = count // PATCH
    inputs = (
        embedded.reshape(patches, PATCH, -1)
        + position_table.astype(jnp.float32)[None]
        + projected.astype(jnp.float32)[:, None, :]
    )
    inputs = inputs.reshape(count, -1)
    inverse = lax.rsqrt(jnp.mean(inputs * inputs, axis=1, keepdims=True) + 1e-06)
    normed = (inputs * inverse * norm_gain).astype(jnp.bfloat16)
    lowered = jnp.dot(normed, local_down, preferred_element_type=jnp.float32)
    byte_tasks = jnp.repeat(tasks, PATCH)
    scales = select_rows(local_scales, byte_tasks)
    shrunk = (lowered * scales).astype(jnp.bfloat16)
    return (inputs, inverse, normed, lowered, scales, shrunk, byte_tasks)


def keep_state(current):
    return current


def update_state(state, query_rows, first, key_heads, value_heads, key_places, scale):
    running_max, running_sum, running_out = state
    count = query_rows.shape[0]
    heads = key_heads.shape[1]
    query_heads = query_rows.reshape(count, heads, HEAD)
    scores = (
        jnp.einsum("qhd,khd->hqk", query_heads, key_heads, preferred_element_type=jnp.float32)
        * scale
    )
    query_places = first + jnp.arange(count, dtype=jnp.int32)
    allowed = key_places[None, :] <= query_places[:, None]
    scores = jnp.where(allowed[None], scores, -1e30)
    new_max = jnp.maximum(running_max, jnp.max(scores, axis=2))
    weights = jnp.where(allowed[None], jnp.exp(scores - new_max[:, :, None]), 0.0)
    shrink = jnp.exp(running_max - new_max)
    running_sum = running_sum * shrink + jnp.sum(weights, axis=2)
    mixed = jnp.einsum(
        "hqk,khd->qhd",
        weights.astype(jnp.bfloat16),
        value_heads,
        preferred_element_type=jnp.float32,
    )
    running_out = running_out * jnp.transpose(shrink)[:, :, None] + mixed
    return (new_max, running_sum, running_out)


def finish_state(state):
    running_max, running_sum, running_out = state
    result = running_out / jnp.transpose(running_sum)[:, :, None]
    return result.reshape(result.shape[0], -1).astype(jnp.bfloat16)


def body(
    patch_queries,
    patch_keys,
    patch_values,
    patch_tasks,
    residual,
    output_weight,
    global_down,
    global_up,
    global_scales,
    local_weight,
    byte_ids,
    byte_table,
    position_table,
    norm_gain,
    hidden_in,
    hidden_out,
    local_down,
    local_up,
    local_scales,
    cotangent,
):
    rows = patch_queries.shape[0]
    width = patch_queries.shape[1]
    heads = width // HEAD
    row_count = lax.axis_size("row")
    seq_index = lax.axis_index("seq")
    row_index = lax.axis_index("row")
    scale = 1.0 / math.sqrt(HEAD)
    own_first = seq_index * rows
    groups = [(patch_queries, own_first)]

    def visit(state, query_rows, first, key_heads, value_heads, key_places):

        def refresh(current):
            return update_state(
                current, query_rows, first, key_heads, value_heads, key_places, scale
            )

        return lax.cond(
            key_places[0] <= first + query_rows.shape[0] - 1, refresh, keep_state, state
        )

    initial = tuple(
        (
            (
                jnp.full((heads, query_rows.shape[0]), -1e30, jnp.float32),
                jnp.zeros((heads, query_rows.shape[0]), jnp.float32),
                jnp.zeros((query_rows.shape[0], heads, HEAD), jnp.float32),
            )
            for query_rows, first in groups
        )
    )
    key_piece = lax.all_gather(patch_keys, "seq", axis=0, tiled=True)
    value_piece = lax.all_gather(patch_values, "seq", axis=0, tiled=True)
    count = key_piece.shape[0]
    span = math.gcd(count, 1024)

    def one_span(index, states):
        offset = index * span
        key_heads = lax.dynamic_slice_in_dim(key_piece, offset, span, 0).reshape(span, heads, HEAD)
        value_heads = lax.dynamic_slice_in_dim(value_piece, offset, span, 0).reshape(
            span, heads, HEAD
        )
        key_places = offset + jnp.arange(span, dtype=jnp.int32)
        updated = []
        for (query_rows, first), state in zip(groups, states):
            updated.append(visit(state, query_rows, first, key_heads, value_heads, key_places))
        return tuple(updated)

    states = lax.fori_loop(0, count // span, one_span, initial)
    outputs = [finish_state(state) for state in states]
    attended = outputs[0]
    reduced = lax.psum(jnp.dot(attended, global_down, preferred_element_type=jnp.float32), "row")
    task_scales = select_rows(global_scales, patch_tasks)
    scaled = (reduced * task_scales).astype(jnp.bfloat16)
    mixed = lax.psum_scatter(
        contract(output_weight, attended, 0, 1).astype(jnp.bfloat16),
        "row",
        scatter_dimension=0,
        tiled=True,
    ).astype(jnp.float32)
    mixed = mixed + jnp.transpose(residual.astype(jnp.float32)) + contract(global_up, scaled, 0, 1)
    mixed_b = mixed.astype(jnp.bfloat16)
    own_patches = rows // row_count
    own_bytes = own_patches * PATCH
    rows_in, rows_out = (
        lax.all_gather(hidden_in, "seq", axis=1, tiled=True),
        lax.all_gather(hidden_out, "seq", axis=1, tiled=True),
    )
    partial_value = contract(mixed_b, local_weight, 0, 0)
    projected = lax.psum(partial_value.astype(jnp.bfloat16), "row")
    every = local_inputs(
        byte_ids,
        projected,
        patch_tasks,
        byte_table,
        position_table,
        norm_gain,
        local_down,
        local_scales,
    )
    normed_all = every[2]
    shrunk_all = every[5]
    cotangent_all = lax.all_gather(cotangent, "row", axis=0, tiled=True)
    inputs, inverse, normed, lowered, scales, shrunk, byte_tasks = [
        lax.dynamic_slice_in_dim(value, row_index * own_bytes, own_bytes, 0) for value in every
    ]
    upper = contract(normed_all, rows_in, 1, 1) + jnp.dot(
        shrunk_all, local_up, preferred_element_type=jnp.float32
    )
    through = contract(cotangent_all, rows_out, 1, 1)
    grown = (through * gelu_slope(upper)).astype(jnp.bfloat16)
    grad_local_up = contract(shrunk_all, grown, 0, 0)
    back_norm, back_rank = (
        lax.psum_scatter(
            jnp.dot(grown, rows_in, preferred_element_type=jnp.float32).astype(jnp.bfloat16),
            "row",
            scatter_dimension=0,
            tiled=True,
        ).astype(jnp.float32),
        lax.psum_scatter(
            contract(grown, local_up, 1, 1).astype(jnp.bfloat16),
            "row",
            scatter_dimension=0,
            tiled=True,
        ).astype(jnp.float32),
    )
    grad_local_scales = task_totals(byte_tasks, back_rank * lowered)
    moved = (back_rank * scales).astype(jnp.bfloat16)
    grad_local_down = contract(normed, moved, 0, 0)
    back_total = back_norm + contract(moved, local_down, 1, 1)
    gained = back_total * norm_gain
    average = jnp.mean(gained * inputs, axis=1, keepdims=True)
    back_inputs = cotangent.astype(jnp.float32) + inverse * (
        gained - inputs * inverse * inverse * average
    )
    patch_grad = back_inputs.reshape(own_patches, PATCH, -1).sum(axis=1).astype(jnp.bfloat16)
    back_mixed = contract(
        lax.all_gather(patch_grad, "row", axis=0, tiled=True), local_weight, 1, 1
    ).astype(jnp.bfloat16)
    grad_global_up = contract(scaled, back_mixed, 0, 0)
    back_scaled = lax.psum(contract(back_mixed, global_up, 1, 1), "row")
    grad_global_scales = task_totals(patch_tasks, back_scaled * reduced)
    back_reduced = (back_scaled * task_scales).astype(jnp.bfloat16)
    grad_global_down = contract(attended, back_reduced, 0, 0)
    grad_global_down, grad_global_up, grad_global_scales, grad_local_up = lax.psum(
        (grad_global_down, grad_global_up, grad_global_scales, grad_local_up), "seq"
    )
    grad_local_down, grad_local_scales = lax.psum(
        (grad_local_down, grad_local_scales), ("seq", "row")
    )
    return (
        grad_global_down,
        grad_global_up,
        grad_global_scales,
        grad_local_down,
        grad_local_up,
        grad_local_scales,
    )


def solution(mesh):
    placed = (
        P("seq", "row"),
        P("seq", "row"),
        P("seq", "row"),
        P("seq"),
        P("seq", "row"),
        P("row", None),
        P("row", None),
        P(None, "row"),
        P(),
        P("row", None),
        P("seq"),
        P(),
        P(),
        P(),
        P("row", "seq"),
        P("row", "seq"),
        P(),
        P(None, "row"),
        P(),
        P(("seq", "row"), None),
    )
    return jax.shard_map(
        body,
        mesh=mesh,
        in_specs=placed,
        out_specs=(P("row", None), P(None, "row"), P(), P(), P(None, "row"), P()),
        check_vma=False,
    )
```

profile of v0, /device:TPU:0, one launch (start us, length us, event | category | flops | bytes accessed | tf_op | source)
XLA Modules:
  0.0 456.6 jit_solution(17964355863576185190)
XLA Ops:
  7.2 1.9 copy.32
  9.2 1.8 copy.33
  11.1 54.3 %all-gather.6.cloned.1.call-done = bf16[2048,1024]{0,1:T(8,128)(2,1)} async-done(((bf16[128,1024]{0,1:T(8,128)(2,1)}), bf16[2048,1024]{0,1:T(8,128)(2,1)}) %all-gather.6.cloned.1.call-update) | async-done | bytes 4194320 | tf_op jit(solution)/shard_map/all_gather | solution.py:150
  65.4 52.8 %all-gather.8.cloned.1.call-done = bf16[2048,1024]{0,1:T(8,128)(2,1)} async-done(((bf16[128,1024]{0,1:T(8,128)(2,1)}), bf16[2048,1024]{0,1:T(8,128)(2,1)}) %all-gather.8.cloned.1.call-update) | async-done | bytes 4194320 | tf_op jit(solution)/shard_map/all_gather | solution.py:151
  118.3 9.3 %while.19 = (s32[]{:T(128)}, f32[8,128]{1,0:T(8,128)S(1)}, f32[8,128]{1,0:T(8,128)S(1)}, f32[128,8,128]{2,0,1:T(8,128)S(1)}, s32[]{:T(128)}, /*index=5*/s32[]{:T...) while((s32[]{:T(128)}, f32[8,128]{1,0:T(8,128)S(1)}, ...), condition=%wide.region_5.6_spmd, body=%wide.region_0.5_spmd.sunk | while | flops 550899840 | bytes 28124504 | solution.py:167
  118.3 0.5 slice.10
  119.5 6.9 %conditional.2 = ((f32[8,128]{1,0:T(8,128)S(1)}, f32[8,128]{1,0:T(8,128)S(1)}, f32[128,8,128]{2,0,1:T(8,128)S(1)})) conditional(s32[]{:T(128)} %convert_element_type.155, (f32[8,128]{1,0:T(8,128)S(1)}, f32[8,128]{1,0:T(8,128)S(1)}, f32[128,8,128]{2,0,1:T(8,128)S(1)}) %tuple.65, (s32[1024]{0:T(1024)S(1)}, s32[]{:T(128)}, s32[]{:T(128)}, ...), branch_computations={%region_1.0_spmd, %region_2.4_spmd} | conditional | flops 550898816 | bytes 28120166 | solution.py:136
  119.5 2.7 constant_dynamic-slice_fusion
  122.3 0.2 broadcast_compare_fusion
  122.5 1.1 fusion
  123.6 1.7 fusion.13
  125.3 1.0 fusion.2
  126.4 0.5 slice.10
  127.7 0.2 copy.34
  127.9 0.1 divide_convert_fusion
  128.0 3.7 fusion.29
  131.8 0.5 all-gather.10.cloned.1.call-update
  132.4 0.5 all-gather.12.cloned.1.call-update
  133.0 0.2 fusion.65
  133.1 5.0 %psum.63 = f32[128,16]{0,1:T(8,128)S(1)} all-reduce(f32[128,16]{0,1:T(8,128)S(1)} %fusion.65), channel_id=1, replica_groups=mesh['seq'=16,'row'=2] {'row'}, use_global_device_ids=true, to_apply=%region_7.8 | all-reduce | flops 2048 | bytes 16384 | tf_op jit(solution)/shard_map/psum | solution.py:170
  138.1 0.8 multiply_convert_fusion.3
  139.0 12.6 %reduce-scatter.4.cloned.1.call-done = bf16[1024,128]{0,1:T(8,128)(2,1)} async-done(((bf16[2048,128]{0,1:T(8,128)(2,1)}), bf16[1024,128]{0,1:T(8,128)(2,1)}) %reduce-scatter.4.cloned.1.call-update) | async-done | bytes 262160 | tf_op jit(solution)/shard_map/reduce_scatter | solution.py:173
  151.6 2.1 fusion.34
  153.7 0.7 all-gather.14.cloned.1.call-update
  154.5 0.1 eq.29
  154.6 0.1 eq.32
  154.7 0.5 fusion.40
  155.2 19.1 %all-gather.10.cloned.1.call-done = bf16[1024,512]{1,0:T(8,128)(2,1)} async-done(((bf16[512,512]{1,0:T(8,128)(2,1)}), bf16[1024,512]{1,0:T(8,128)(2,1)}) %all-gather.10.cloned.1.call-update) | async-done | bytes 1048592 | tf_op jit(solution)/shard_map/all_gather | solution.py:201
  174.3 39.9 %all-gather.12.cloned.1.call-done = bf16[1024,512]{0,1:T(8,128)(2,1)} async-done(((bf16[1024,32]{0,1:T(8,128)(2,1)}), bf16[1024,512]{0,1:T(8,128)(2,1)}) %all-gather.12.cloned.1.call-update) | async-done | bytes 1048592 | tf_op jit(solution)/shard_map/all_gather | solution.py:185
  214.2 4.7 %fusion.60 = f32[1024,1024]{1,0:T(8,128)} fusion(bf16[1024,512]{1,0:T(8,128)(2,1)} %all-gather.10.cloned.1.call-done, bf16[1024,512]{0,1:T(8,128)(2,1)} %all-gather.12.cloned.1.call-done), kind=kOutput, calls=%fused_computation.86 | convolution fusion | flops 1073741824 | bytes 6291456 | tf_op jit(solution)/shard_map/dot_general | solution.py:14
  218.9 17.9 %all-reduce.5.cloned.1.call-done = bf16[128,512]{1,0:T(8,128)(2,1)} async-done(((bf16[128,512]{1,0:T(8,128)(2,1)}), bf16[128,512]{1,0:T(8,128)(2,1)}) %all-reduce.5.cloned.1.call-update) | async-done | bytes 131088 | tf_op jit(solution)/shard_map/psum | solution.py:188
  236.8 0.9 convert_element_type.97
  237.7 1.6 multiply_reduce_fusion
  239.4 0.6 copy-done.9
  240.0 0.2 multiply_convert_fusion
  240.2 1.0 copy-done.3
  241.2 1.0 multiply_convert_fusion.1
  242.3 34.6 %all-gather.14.cloned.1.call-done = bf16[1024,512]{0,1:T(8,128)(2,1)} async-done(((bf16[1024,32]{0,1:T(8,128)(2,1)}), bf16[1024,512]{0,1:T(8,128)(2,1)}) %all-gather.14.cloned.1.call-update) | async-done | bytes 1048592 | tf_op jit(solution)/shard_map/all_gather | solution.py:184
  276.8 2.9 fusion.61
  279.8 2.3 fusion.28
  282.1 1.3 copy-done.1
  283.4 1.3 convolution_convert_fusion.3
  284.7 0.2 reduce-scatter.6.cloned.1.call-start
  284.9 4.1 convolution_convert_fusion.1
  289.2 1.3 dynamic_slice.47
  290.5 1.3 dynamic-slice.3
  291.8 2.6 fusion.64
  294.4 1.8 fusion.43
  296.2 1.2 fusion.36
  297.4 40.2 %all-reduce = (f32[512,16]{0,1:T(8,128)}, f32[8,16]{1,0:T(8,128)}) all-reduce(f32[512,16]{0,1:T(8,128)S(1)} %fusion.36, f32[8,16]{1,0:T(8,128)} %fusion.43), channel_id=1, replica_groups=mesh['seq'=16,'row'=2] {'seq','row'}, use_global_device_ids=true, to_apply=%region_18.19 | all-reduce | flops 8320 | bytes 66560 | tf_op jit(solution)/shard_map/psum | solution.py:246
  337.7 1.5 multiply_reduce_fusion.1
  339.2 1.6 bitcast_reduce_fusion
  340.8 5.2 %all_gather.23 = bf16[128,512]{1,0:T(8,128)(2,1)S(1)} all-gather(bf16[64,512]{1,0:T(8,128)(2,1)S(1)} %bitcast_reduce_fusion), channel_id=1, replica_groups=mesh['seq'=16,'row'=2] {'row'}, dimensions={0}, use_global_device_ids=true | all-gather | bytes 196608 | tf_op jit(solution)/shard_map/all_gather | solution.py:236
  346.0 0.5 convolution_convert_fusion.2
  346.5 0.2 fusion.62
  346.7 0.8 fusion.63
  347.5 5.0 %psum.65 = f32[128,16]{0,1:T(8,128)S(1)} all-reduce(f32[128,16]{0,1:T(8,128)S(1)} %fusion.62), channel_id=1, replica_groups=mesh['seq'=16,'row'=2] {'row'}, use_global_device_ids=true, to_apply=%region_14.15 | all-reduce | flops 2048 | bytes 16384 | tf_op jit(solution)/shard_map/psum | solution.py:239
  352.4 0.8 fusion.55
  353.3 0.2 fusion.49
  353.5 30.1 %psum.68 = f32[8,16]{1,0:T(8,128)} all-reduce(f32[8,16]{1,0:T(8,128)S(1)} %fusion.49), channel_id=1, replica_groups=mesh['seq'=16,'row'=2] {'seq'}, use_global_device_ids=true, to_apply=%region_17.18 | all-reduce | flops 128 | bytes 1024 | tf_op jit(solution)/shard_map/psum | solution.py:243
  383.6 61.7 %all-reduce.7.cloned.1.call-done = (f32[1024,16]{0,1:T(8,128)}, f32[16,1024]{1,0:T(8,128)}, f32[16,1024]{1,0:T(8,128)}) async-done(((f32[1024,16]{0,1:T(8,128)}, f32[16,1024]{1,0:T(8,128)}, f32[16,1024]{1,0:T(8,128)}), (f32[1024,16]{0,1:T(8,128)}, f32[16,1024]{1,0:T(8,128)}, f32[16,1024]{1,0:T(8,128)})) %all-reduce.7.cloned.1.call-update) | async-done | bytes 196624 | tf_op jit(solution)/shard_map/psum | solution.py:243
  445.3 1.5 copy.67
  446.8 1.5 copy.68
  448.3 1.5 copy.69
  (74 shorter events, 0.7 us)
Async XLA Ops:
  7.2 144.4 %copy-start = (bf16[1024,512]{1,0:T(8,128)(2,1)S(1)}, bf16[1024,512]{1,0:T(8,128)(2,1)}, u32[]{:S(2)}) copy-start(bf16[1024,512]{1,0:T(8,128)(2,1)} %param.33) | copy-start | bytes 3145732
  7.2 58.2 %all-gather.6.cloned.1.call-start = ((), (), s32[]{:S(2)}) async-start(), calls=%async_computation.3 | async-start | bytes 4456448 | tf_op jit(solution)/shard_map/all_gather | solution.py:150
  9.1 109.1 %all-gather.8.cloned.1.call-start = ((), (), s32[]{:S(2)}) async-start(), calls=%async_computation.4 | async-start | bytes 4456448 | tf_op jit(solution)/shard_map/all_gather | solution.py:151
  11.0 140.6 %reduce-scatter.4.cloned.1.call-start = ((), (), s32[]{:S(2)}) async-start(), calls=%async_computation.5 | async-start | bytes 786432 | tf_op jit(solution)/shard_map/reduce_scatter | solution.py:173
  119.5 3.0 copy-start.2
  127.6 5.3 %copy-start.8 = (bf16[1024,16]{0,1:T(8,128)(2,1)S(1)}, bf16[1024,16]{0,1:T(8,128)(2,1)}, u32[]{:S(2)}) copy-start(bf16[1024,16]{0,1:T(8,128)(2,1)} %param.30) | copy-start | bytes 98308
  127.6 10.5 %copy-start.18 = (s32[128]{0:T(128)S(1)}, s32[128]{0:T(128)}, u32[]{:S(2)}) copy-start(s32[128]{0:T(128)} %param.27) | copy-start | bytes 1540
  127.6 10.5 %copy-start.20 = (f32[8,16]{1,0:T(8,128)S(1)}, f32[8,16]{1,0:T(8,128)}, u32[]{:S(2)}) copy-start(f32[8,16]{1,0:T(8,128)} %param.32) | copy-start | bytes 1540
  127.7 23.9 %copy-start.4 = (bf16[128,1024]{1,0:T(8,128)(2,1)S(1)}, bf16[128,1024]{1,0:T(8,128)(2,1)}, u32[]{:S(2)}) copy-start(bf16[128,1024]{1,0:T(8,128)(2,1)} %param.28) | copy-start | bytes 786436
  127.7 23.9 %copy-start.5 = (bf16[16,1024]{1,0:T(8,128)(2,1)S(1)}, bf16[16,1024]{1,0:T(8,128)(2,1)}, u32[]{:S(2)}) copy-start(bf16[16,1024]{1,0:T(8,128)(2,1)} %param.31) | copy-start | bytes 98308
  127.9 26.5 %copy-start.13 = (bf16[8,512]{1,0:T(8,128)(2,1)S(1)}, bf16[8,512]{1,0:T(8,128)(2,1)}, u32[]{:S(2)}) copy-start(bf16[8,512]{1,0:T(8,128)(2,1)} %param.36) | copy-start | bytes 24580
  128.0 26.7 %copy-start.21 = (f32[8,16]{1,0:T(8,128)S(1)}, f32[8,16]{1,0:T(8,128)}, u32[]{:S(2)}) copy-start(f32[8,16]{1,0:T(8,128)} %param.42) | copy-start | bytes 1540
  131.7 42.6 %all-gather.10.cloned.1.call-start = ((), (), s32[]{:S(2)}) async-start(), calls=%async_computation.7 | async-start | bytes 1572864 | tf_op jit(solution)/shard_map/all_gather | solution.py:201
  132.3 81.9 %all-gather.12.cloned.1.call-start = ((), (), s32[]{:S(2)}) async-start(), calls=%async_computation.8 | async-start | bytes 1114112 | tf_op jit(solution)/shard_map/all_gather | solution.py:185
  132.9 103.9 %all-reduce.5.cloned.1.call-start = ((), (), s32[]{:S(2)}) async-start(), calls=%async_computation.6 | async-start | bytes 262144 | tf_op jit(solution)/shard_map/psum | solution.py:188
  138.1 80.8 %copy-start.15 = (f32[128,16]{0,1:T(8,128)}, f32[128,16]{0,1:T(8,128)S(1)}, u32[]{:S(2)}) copy-start(f32[128,16]{0,1:T(8,128)S(1)} %psum.63) | copy-start | bytes 24580
  139.0 15.6 %copy-start.10 = (bf16[128,16]{0,1:T(8,128)(2,1)}, bf16[128,16]{0,1:T(8,128)(2,1)S(1)}, u32[]{:S(2)}) copy-start(bf16[128,16]{0,1:T(8,128)(2,1)S(1)} %get-tuple-element.359) | copy-start | bytes 12292
  153.7 123.2 %all-gather.14.cloned.1.call-start = ((), (), s32[]{:S(2)}) async-start(), calls=%async_computation.9 | async-start | bytes 1114112 | tf_op jit(solution)/shard_map/all_gather | solution.py:184
  154.4 140.0 %reduce-scatter.8.cloned.1.call-start = ((), (), s32[]{:S(2)}) async-start(), calls=%async_computation.11 | async-start | bytes 49152 | tf_op jit(solution)/shard_map/reduce_scatter | solution.py:218
  154.7 64.2 %copy-start.12 = (s32[1024]{0:T(1024)}, s32[1024]{0:T(1024)S(1)}, u32[]{:S(2)}) copy-start(s32[1024]{0:T(1024)S(1)} %eq.32) | copy-start | bytes 12292
  155.2 84.8 %copy-start.17 = (f32[512]{0:T(512)S(1)}, f32[512]{0:T(512)}, u32[]{:S(2)}) copy-start(f32[512]{0:T(512)} %param.37) | copy-start | bytes 6148
  218.9 22.3 %copy-start.6 = (bf16[512,16]{0,1:T(8,128)(2,1)S(1)}, bf16[512,16]{0,1:T(8,128)(2,1)}, u32[]{:S(2)}) copy-start(bf16[512,16]{0,1:T(8,128)(2,1)} %param.40) | copy-start | bytes 49156
  239.4 0.6 copy-start.9
  240.2 1.0 copy-start.3
  276.8 3.0 copy-start.7
  276.8 3.0 copy-start.22
  282.1 1.3 copy-start.1
  284.7 52.9 %reduce-scatter.6.cloned.1.call-start = ((), (), s32[]{:S(2)}) async-start(), calls=%async_computation.10 | async-start | bytes 1572864 | tf_op jit(solution)/shard_map/reduce_scatter | solution.py:212
  289.1 156.2 %all-reduce.7.cloned.1.call-start = ((), (), s32[]{:S(2)}) async-start(), calls=%async_computation.12 | async-start | bytes 393216 | tf_op jit(solution)/shard_map/psum | solution.py:243
  337.6 9.0 %copy-start.11 = (bf16[128,16]{0,1:T(8,128)(2,1)S(1)}, bf16[128,16]{0,1:T(8,128)(2,1)}, u32[]{:S(2)}) copy-start(bf16[128,16]{0,1:T(8,128)(2,1)} %copy-done.10) | copy-start | bytes 12292
  337.6 14.8 %copy-start.14 = (f32[128,16]{0,1:T(8,128)S(1)}, f32[128,16]{0,1:T(8,128)}, u32[]{:S(2)}) copy-start(f32[128,16]{0,1:T(8,128)} %get-tuple-element.360) | copy-start | bytes 24580
  337.6 15.7 %copy-start.16 = (f32[128,16]{0,1:T(8,128)S(1)}, f32[128,16]{0,1:T(8,128)}, u32[]{:S(2)}) copy-start(f32[128,16]{0,1:T(8,128)} %copy-done.15) | copy-start | bytes 24580
  337.6 15.7 %copy-start.19 = (s32[128]{0:T(128)S(1)}, s32[128]{0:T(128)}, u32[]{:S(2)}) copy-start(s32[128]{0:T(128)} %param.27) | copy-start | bytes 1540
Sparse Core Ops, SparseCore 0:
  10.1 55.1 all-gather.5
  67.5 50.6 all-gather.7
  131.9 19.6 reduce-scatter.3
  153.0 21.2 all-gather.9
  176.3 37.8 all-gather.11
  216.3 20.4 all-reduce.4
  239.0 37.8 all-gather.13
  284.8 8.9 reduce-scatter.7
  296.1 20.9 reduce-scatter.5
  353.4 91.8 all-reduce.6
where the time goes:
time: 457 us
  waiting for transfers between devices  295 us (65%)
  blocking collectives  85.4 us (19%)
  matrix products  37.7 us (8%)
  local copies, waits for them, and re-layouts  17.9 us (4%)
  between operations  14.5 us (3%)
    psum x1, waiting for transfers between devices, body(): lax.psum((grad_global_down, grad_global_up, grad_global_scales, grad_loca...  61.7 us
    all_gather x1, waiting for transfers between devices, body(): key_piece = lax.all_gather(patch_keys, 'seq', axis=0, tiled=True)  54.3 us
    all_gather x1, waiting for transfers between devices, body(): value_piece = lax.all_gather(patch_values, 'seq', axis=0, tiled=True)  52.8 us
    psum x1, blocking collectives, body(): lax.psum((grad_local_down, grad_local_scales), ('seq', 'row'))  40.2 us
    all_gather x1, waiting for transfers between devices, body(): lax.all_gather(hidden_out, 'seq', axis=1, tiled=True)  39.9 us
    all_gather x1, waiting for transfers between devices, body(): lax.all_gather(hidden_in, 'seq', axis=1, tiled=True)  34.6 us
    psum x1, blocking collectives, body(): lax.psum((grad_global_down, grad_global_up, grad_global_scales, grad_loca...  30.1 us
    dot_general x12, matrix products, contract(): lax.dot_general(left, right, (((left_dim,), (right_dim,)), ((), ())), pre...  22.4 us
  transfers between devices with their start and end apart: 10, of which 8 were waited for; matrix products, arithmetic and copies ran while one was open for 6% of the time, Pallas kernels for 0%

commit v1 on v0

--- a/solution.py
+++ b/solution.py
@@ -244,7 +244,7 @@
         (grad_global_down, grad_global_up, grad_global_scales, grad_local_up), "seq"
     )
     grad_local_down, grad_local_scales = lax.psum(
-        (grad_local_down, grad_local_scales), ("seq", "row")
+        lax.psum((grad_local_down, grad_local_scales), "row"), "seq"
     )
     return (
         grad_global_down,

time: 457 us -> 439 us (0.961)
  blocking collectives: 85.4 us -> 76 us
  waiting for transfers between devices: 295 us -> 286 us
    psum x1 -> x0, blocking collectives: 40.2 us -> none  [body(): lax.psum((grad_local_down, grad_local_scales), ('seq', 'row'))]
    psum x1, blocking collectives: 30.1 us -> 58.6 us  [body(): lax.psum((grad_global_down, grad_global_up, grad_global_scales, grad_loca...]
    psum x1, waiting for transfers between devices: 61.7 us -> 34 us  [body(): lax.psum((grad_global_down, grad_global_up, grad_global_scales, grad_loca...]
    reduce_scatter x1, waiting for transfers between devices: 0.02 us -> 19.1 us  [body(): lax.psum_scatter(jnp.dot(grown, rows_in, preferred_element_type=jnp.float...]
    unnamed x49 -> x51, local copies, waits for them, and re-layouts: 11.1 us -> 11.1 us
  transfers between devices with their start and end apart: 10 -> 10, of which waited for: 8 -> 9; matrix products, arithmetic and copies ran while one was open for 6% -> 6% of each run, Pallas kernels for 0% -> 0%
where the time goes in v1:
time: 439 us
  waiting for transfers between devices  286 us (65%)
  blocking collectives  76 us (17%)
  matrix products  37.8 us (9%)
  local copies, waits for them, and re-layouts  18 us (4%)
  between operations  14.5 us (3%)
    psum x1, blocking collectives, body(): lax.psum((grad_global_down, grad_global_up, grad_global_scales, grad_loca...  58.6 us
    all_gather x1, waiting for transfers between devices, body(): key_piece = lax.all_gather(patch_keys, 'seq', axis=0, tiled=True)  54.3 us
    all_gather x1, waiting for transfers between devices, body(): value_piece = lax.all_gather(patch_values, 'seq', axis=0, tiled=True)  52.8 us
    all_gather x1, waiting for transfers between devices, body(): lax.all_gather(hidden_out, 'seq', axis=1, tiled=True)  39.9 us
    all_gather x1, waiting for transfers between devices, body(): lax.all_gather(hidden_in, 'seq', axis=1, tiled=True)  34.6 us
    psum x1, waiting for transfers between devices, body(): lax.psum((grad_global_down, grad_global_up, grad_global_scales, grad_loca...  34 us
    dot_general x12, matrix products, contract(): lax.dot_general(left, right, (((left_dim,), (right_dim,)), ((), ())), pre...  22.4 us
    all_gather x1, waiting for transfers between devices, body(): cotangent_all = lax.all_gather(cotangent, 'row', axis=0, tiled=True)  19.1 us
  transfers between devices with their start and end apart: 10, of which 9 were waited for; matrix products, arithmetic and copies ran while one was open for 6% of the time, Pallas kernels for 0%

profile of v1, /device:TPU:0, one launch (start us, length us, event | category | flops | bytes accessed | tf_op | source)
XLA Modules:
  0.0 438.6 jit_solution(9618418370625930633)
XLA Ops:
  7.2 1.9 copy.32
  9.2 1.8 copy.33
  11.1 54.3 %all-gather.6.cloned.1.call-done = bf16[2048,1024]{0,1:T(8,128)(2,1)} async-done(((bf16[128,1024]{0,1:T(8,128)(2,1)}), bf16[2048,1024]{0,1:T(8,128)(2,1)}) %all-gather.6.cloned.1.call-update) | async-done | bytes 4194320 | tf_op jit(solution)/shard_map/all_gather | solution.py:150
  65.4 52.8 %all-gather.8.cloned.1.call-done = bf16[2048,1024]{0,1:T(8,128)(2,1)} async-done(((bf16[128,1024]{0,1:T(8,128)(2,1)}), bf16[2048,1024]{0,1:T(8,128)(2,1)}) %all-gather.8.cloned.1.call-update) | async-done | bytes 4194320 | tf_op jit(solution)/shard_map/all_gather | solution.py:151
  118.3 9.3 %while.19 = (s32[]{:T(128)}, f32[8,128]{1,0:T(8,128)S(1)}, f32[8,128]{1,0:T(8,128)S(1)}, f32[128,8,128]{2,0,1:T(8,128)S(1)}, s32[]{:T(128)}, /*index=5*/s32[]{:T...) while((s32[]{:T(128)}, f32[8,128]{1,0:T(8,128)S(1)}, ...), condition=%wide.region_5.6_spmd, body=%wide.region_0.5_spmd.sunk | while | flops 550899840 | bytes 28124504 | solution.py:167
  118.3 0.5 slice.10
  119.5 6.9 %conditional.2 = ((f32[8,128]{1,0:T(8,128)S(1)}, f32[8,128]{1,0:T(8,128)S(1)}, f32[128,8,128]{2,0,1:T(8,128)S(1)})) conditional(s32[]{:T(128)} %convert_element_type.155, (f32[8,128]{1,0:T(8,128)S(1)}, f32[8,128]{1,0:T(8,128)S(1)}, f32[128,8,128]{2,0,1:T(8,128)S(1)}) %tuple.65, (s32[1024]{0:T(1024)S(1)}, s32[]{:T(128)}, s32[]{:T(128)}, ...), branch_computations={%region_1.0_spmd, %region_2.4_spmd} | conditional | flops 550898816 | bytes 28120166 | solution.py:136
  119.5 2.7 constant_dynamic-slice_fusion
  122.3 0.2 broadcast_compare_fusion
  122.5 1.1 fusion
  123.6 1.7 fusion.13
  125.3 1.0 fusion.2
  126.4 0.5 slice.10
  127.7 0.2 copy.34
  127.9 0.1 divide_convert_fusion
  128.0 3.8 fusion.29
  131.8 0.5 all-gather.10.cloned.1.call-update
  132.4 0.5 all-gather.12.cloned.1.call-update
  133.0 0.2 fusion.65
  133.1 5.0 %psum.77 = f32[128,16]{0,1:T(8,128)S(1)} all-reduce(f32[128,16]{0,1:T(8,128)S(1)} %fusion.65), channel_id=1, replica_groups=mesh['seq'=16,'row'=2] {'row'}, use_global_device_ids=true, to_apply=%region_7.8 | all-reduce | flops 2048 | bytes 16384 | tf_op jit(solution)/shard_map/psum | solution.py:170
  138.1 0.9 multiply_convert_fusion.3
  139.0 12.6 %reduce-scatter.4.cloned.1.call-done = bf16[1024,128]{0,1:T(8,128)(2,1)} async-done(((bf16[2048,128]{0,1:T(8,128)(2,1)}), bf16[1024,128]{0,1:T(8,128)(2,1)}) %reduce-scatter.4.cloned.1.call-update) | async-done | bytes 262160 | tf_op jit(solution)/shard_map/reduce_scatter | solution.py:173
  151.6 2.1 fusion.34
  153.7 0.7 all-gather.14.cloned.1.call-update
  154.5 0.1 eq.29
  154.6 0.1 eq.32
  154.7 0.5 fusion.40
  155.2 19.1 %all-gather.10.cloned.1.call-done = bf16[1024,512]{1,0:T(8,128)(2,1)} async-done(((bf16[512,512]{1,0:T(8,128)(2,1)}), bf16[1024,512]{1,0:T(8,128)(2,1)}) %all-gather.10.cloned.1.call-update) | async-done | bytes 1048592 | tf_op jit(solution)/shard_map/all_gather | solution.py:201
  174.3 39.9 %all-gather.12.cloned.1.call-done = bf16[1024,512]{0,1:T(8,128)(2,1)} async-done(((bf16[1024,32]{0,1:T(8,128)(2,1)}), bf16[1024,512]{0,1:T(8,128)(2,1)}) %all-gather.12.cloned.1.call-update) | async-done | bytes 1048592 | tf_op jit(solution)/shard_map/all_gather | solution.py:185
  214.2 4.7 %fusion.60 = f32[1024,1024]{1,0:T(8,128)} fusion(bf16[1024,512]{1,0:T(8,128)(2,1)} %all-gather.10.cloned.1.call-done, bf16[1024,512]{0,1:T(8,128)(2,1)} %all-gather.12.cloned.1.call-done), kind=kOutput, calls=%fused_computation.86 | convolution fusion | flops 1073741824 | bytes 6291456 | tf_op jit(solution)/shard_map/dot_general | solution.py:14
  218.9 17.9 %all-reduce.6.cloned.1.call-done = bf16[128,512]{1,0:T(8,128)(2,1)} async-done(((bf16[128,512]{1,0:T(8,128)(2,1)}), bf16[128,512]{1,0:T(8,128)(2,1)}) %all-reduce.6.cloned.1.call-update) | async-done | bytes 131088 | tf_op jit(solution)/shard_map/psum | solution.py:188
  236.8 0.9 convert_element_type.97
  237.8 1.6 multiply_reduce_fusion
  239.4 0.6 copy-done.9
  240.0 0.2 multiply_convert_fusion
  240.3 1.0 copy-done.3
  241.2 1.0 multiply_convert_fusion.1
  242.3 34.6 %all-gather.14.cloned.1.call-done = bf16[1024,512]{0,1:T(8,128)(2,1)} async-done(((bf16[1024,32]{0,1:T(8,128)(2,1)}), bf16[1024,512]{0,1:T(8,128)(2,1)}) %all-gather.14.cloned.1.call-update) | async-done | bytes 1048592 | tf_op jit(solution)/shard_map/all_gather | solution.py:184
  276.9 2.9 fusion.61
  279.8 2.3 fusion.28
  282.1 1.3 copy-done.1
  283.5 1.3 convolution_convert_fusion.3
  284.8 0.2 reduce-scatter.6.cloned.1.call-start
  285.0 4.1 convolution_convert_fusion.1
  289.2 1.3 dynamic_slice.47
  290.5 1.3 dynamic-slice.3
  291.9 2.6 fusion.64
  294.5 1.8 fusion.43
  296.2 1.2 fusion.36
  297.5 19.1 %reduce-scatter.6.cloned.1.call-done = bf16[512,512]{1,0:T(8,128)(2,1)} async-done(((bf16[1024,512]{1,0:T(8,128)(2,1)}), bf16[512,512]{1,0:T(8,128)(2,1)}) %reduce-scatter.6.cloned.1.call-update) | async-done | bytes 524304 | tf_op jit(solution)/shard_map/reduce_scatter | solution.py:212
  316.5 1.5 multiply_reduce_fusion.1
  318.1 1.6 bitcast_reduce_fusion
  319.7 4.9 %all_gather.23 = bf16[128,512]{1,0:T(8,128)(2,1)S(1)} all-gather(bf16[64,512]{1,0:T(8,128)(2,1)S(1)} %bitcast_reduce_fusion), channel_id=1, replica_groups=mesh['seq'=16,'row'=2] {'row'}, dimensions={0}, use_global_device_ids=true | all-gather | bytes 196608 | tf_op jit(solution)/shard_map/all_gather | solution.py:236
  324.7 0.5 convolution_convert_fusion.2
  325.2 0.2 fusion.62
  325.3 0.8 fusion.63
  326.1 7.5 %all-reduce.2 = (f32[128,16]{0,1:T(8,128)S(1)}, f32[512,16]{0,1:T(8,128)S(1)}, f32[8,16]{1,0:T(8,128)S(1)}) all-reduce(f32[128,16]{0,1:T(8,128)S(1)} %fusion.62, f32[512,16]{0,1:T(8,128)S(1)} %fusion.36, f32[8,16]{1,0:T(8,128)S(1)} %copy-done.18), channel_id=1, replica_groups=mesh['seq'=16,'row'=2] {'row'}, use_global_device_ids=true, to_apply=%region_14.15 | all-reduce | flops 10368 | bytes 82944 | tf_op jit(solution)/shard_map/psum | solution.py:239
  333.7 0.8 fusion.55
  334.5 0.2 fusion.49
  334.8 58.6 %all-reduce = (f32[8,16]{1,0:T(8,128)}, f32[512,16]{0,1:T(8,128)}, f32[8,16]{1,0:T(8,128)}) all-reduce(f32[8,16]{1,0:T(8,128)S(1)} %fusion.49, f32[512,16]{0,1:T(8,128)S(1)} %get-tuple-element.355, f32[8,16]{1,0:T(8,128)S(1)} %get-tuple-element.356), channel_id=1, replica_groups=mesh['seq'=16,'row'=2] {'seq'}, use_global_device_ids=true, to_apply=%region_17.18 | all-reduce | flops 8448 | bytes 67584 | tf_op jit(solution)/shard_map/psum | solution.py:243
  393.4 34.0 %all-reduce.8.cloned.1.call-done = (f32[1024,16]{0,1:T(8,128)}, f32[16,1024]{1,0:T(8,128)}, f32[16,1024]{1,0:T(8,128)}) async-done(((f32[1024,16]{0,1:T(8,128)}, f32[16,1024]{1,0:T(8,128)}, f32[16,1024]{1,0:T(8,128)}), (f32[1024,16]{0,1:T(8,128)}, f32[16,1024]{1,0:T(8,128)}, f32[16,1024]{1,0:T(8,128)})) %all-reduce.8.cloned.1.call-update) | async-done | bytes 196624 | tf_op jit(solution)/shard_map/psum | solution.py:243
  427.3 1.5 copy.67
  428.8 1.5 copy.68
  430.3 1.5 copy.69
  (75 shorter events, 0.7 us)
Async XLA Ops:
  7.2 144.4 %copy-start = (bf16[1024,512]{1,0:T(8,128)(2,1)S(1)}, bf16[1024,512]{1,0:T(8,128)(2,1)}, u32[]{:S(2)}) copy-start(bf16[1024,512]{1,0:T(8,128)(2,1)} %param.33) | copy-start | bytes 3145732
  7.2 58.2 %all-gather.6.cloned.1.call-start = ((), (), s32[]{:S(2)}) async-start(), calls=%async_computation.3 | async-start | bytes 4456448 | tf_op jit(solution)/shard_map/all_gather | solution.py:150
  9.1 109.1 %all-gather.8.cloned.1.call-start = ((), (), s32[]{:S(2)}) async-start(), calls=%async_computation.4 | async-start | bytes 4456448 | tf_op jit(solution)/shard_map/all_gather | solution.py:151
  11.0 140.6 %reduce-scatter.4.cloned.1.call-start = ((), (), s32[]{:S(2)}) async-start(), calls=%async_computation.5 | async-start | bytes 786432 | tf_op jit(solution)/shard_map/reduce_scatter | solution.py:173
  119.5 3.0 copy-start.2
  127.6 5.4 %copy-start.8 = (bf16[1024,16]{0,1:T(8,128)(2,1)S(1)}, bf16[1024,16]{0,1:T(8,128)(2,1)}, u32[]{:S(2)}) copy-start(bf16[1024,16]{0,1:T(8,128)(2,1)} %param.30) | copy-start | bytes 98308
  127.6 10.5 %copy-start.19 = (s32[128]{0:T(128)S(1)}, s32[128]{0:T(128)}, u32[]{:S(2)}) copy-start(s32[128]{0:T(128)} %param.27) | copy-start | bytes 1540
  127.6 10.5 %copy-start.21 = (f32[8,16]{1,0:T(8,128)S(1)}, f32[8,16]{1,0:T(8,128)}, u32[]{:S(2)}) copy-start(f32[8,16]{1,0:T(8,128)} %param.32) | copy-start | bytes 1540
  127.7 23.9 %copy-start.4 = (bf16[128,1024]{1,0:T(8,128)(2,1)S(1)}, bf16[128,1024]{1,0:T(8,128)(2,1)}, u32[]{:S(2)}) copy-start(bf16[128,1024]{1,0:T(8,128)(2,1)} %param.28) | copy-start | bytes 786436
  127.7 23.9 %copy-start.5 = (bf16[16,1024]{1,0:T(8,128)(2,1)S(1)}, bf16[16,1024]{1,0:T(8,128)(2,1)}, u32[]{:S(2)}) copy-start(bf16[16,1024]{1,0:T(8,128)(2,1)} %param.31) | copy-start | bytes 98308
  127.9 26.5 %copy-start.13 = (bf16[8,512]{1,0:T(8,128)(2,1)S(1)}, bf16[8,512]{1,0:T(8,128)(2,1)}, u32[]{:S(2)}) copy-start(bf16[8,512]{1,0:T(8,128)(2,1)} %param.36) | copy-start | bytes 24580
  128.0 26.7 %copy-start.22 = (f32[8,16]{1,0:T(8,128)S(1)}, f32[8,16]{1,0:T(8,128)}, u32[]{:S(2)}) copy-start(f32[8,16]{1,0:T(8,128)} %param.42) | copy-start | bytes 1540
  131.8 42.6 %all-gather.10.cloned.1.call-start = ((), (), s32[]{:S(2)}) async-start(), calls=%async_computation.7 | async-start | bytes 1572864 | tf_op jit(solution)/shard_map/all_gather | solution.py:201
  132.3 81.9 %all-gather.12.cloned.1.call-start = ((), (), s32[]{:S(2)}) async-start(), calls=%async_computation.8 | async-start | bytes 1114112 | tf_op jit(solution)/shard_map/all_gather | solution.py:185
  132.9 103.9 %all-reduce.6.cloned.1.call-start = ((), (), s32[]{:S(2)}) async-start(), calls=%async_computation.6 | async-start | bytes 262144 | tf_op jit(solution)/shard_map/psum | solution.py:188
  138.1 80.8 %copy-start.15 = (f32[128,16]{0,1:T(8,128)}, f32[128,16]{0,1:T(8,128)S(1)}, u32[]{:S(2)}) copy-start(f32[128,16]{0,1:T(8,128)S(1)} %psum.77) | copy-start | bytes 24580
  139.0 15.6 %copy-start.10 = (bf16[128,16]{0,1:T(8,128)(2,1)}, bf16[128,16]{0,1:T(8,128)(2,1)S(1)}, u32[]{:S(2)}) copy-start(bf16[128,16]{0,1:T(8,128)(2,1)S(1)} %get-tuple-element.363) | copy-start | bytes 12292
  153.7 123.2 %all-gather.14.cloned.1.call-start = ((), (), s32[]{:S(2)}) async-start(), calls=%async_computation.9 | async-start | bytes 1114112 | tf_op jit(solution)/shard_map/all_gather | solution.py:184
  154.4 140.0 %reduce-scatter.8.cloned.1.call-start = ((), (), s32[]{:S(2)}) async-start(), calls=%async_computation.11 | async-start | bytes 49152 | tf_op jit(solution)/shard_map/reduce_scatter | solution.py:218
  154.7 64.3 %copy-start.12 = (s32[1024]{0:T(1024)}, s32[1024]{0:T(1024)S(1)}, u32[]{:S(2)}) copy-start(s32[1024]{0:T(1024)S(1)} %eq.32) | copy-start | bytes 12292
  155.2 84.8 %copy-start.17 = (f32[512]{0:T(512)S(1)}, f32[512]{0:T(512)}, u32[]{:S(2)}) copy-start(f32[512]{0:T(512)} %param.37) | copy-start | bytes 6148
  218.9 22.3 %copy-start.6 = (bf16[512,16]{0,1:T(8,128)(2,1)S(1)}, bf16[512,16]{0,1:T(8,128)(2,1)}, u32[]{:S(2)}) copy-start(bf16[512,16]{0,1:T(8,128)(2,1)} %param.40) | copy-start | bytes 49156
  239.4 0.6 copy-start.9
  240.3 1.0 copy-start.3
  276.9 3.0 copy-start.7
  276.9 3.0 copy-start.23
  282.1 1.4 copy-start.1
  284.8 31.8 %reduce-scatter.6.cloned.1.call-start = ((), (), s32[]{:S(2)}) async-start(), calls=%async_computation.10 | async-start | bytes 1572864 | tf_op jit(solution)/shard_map/reduce_scatter | solution.py:212
  289.1 138.2 %all-reduce.8.cloned.1.call-start = ((), (), s32[]{:S(2)}) async-start(), calls=%async_computation.12 | async-start | bytes 393216 | tf_op jit(solution)/shard_map/psum | solution.py:243
  316.5 8.8 %copy-start.11 = (bf16[128,16]{0,1:T(8,128)(2,1)S(1)}, bf16[128,16]{0,1:T(8,128)(2,1)}, u32[]{:S(2)}) copy-start(bf16[128,16]{0,1:T(8,128)(2,1)} %copy-done.10) | copy-start | bytes 12292
  318.1 8.1 %copy-start.18 = (f32[8,16]{1,0:T(8,128)S(1)}, f32[8,16]{1,0:T(8,128)}, u32[]{:S(2)}) copy-start(f32[8,16]{1,0:T(8,128)} %fusion.43) | copy-start | bytes 1540
  318.1 15.6 %copy-start.14 = (f32[128,16]{0,1:T(8,128)S(1)}, f32[128,16]{0,1:T(8,128)}, u32[]{:S(2)}) copy-start(f32[128,16]{0,1:T(8,128)} %get-tuple-element.364) | copy-start | bytes 24580
  318.1 16.5 %copy-start.16 = (f32[128,16]{0,1:T(8,128)S(1)}, f32[128,16]{0,1:T(8,128)}, u32[]{:S(2)}) copy-start(f32[128,16]{0,1:T(8,128)} %copy-done.15) | copy-start | bytes 24580
  318.1 16.5 %copy-start.20 = (s32[128]{0:T(128)S(1)}, s32[128]{0:T(128)}, u32[]{:S(2)}) copy-start(s32[128]{0:T(128)} %param.27) | copy-start | bytes 1540
Sparse Core Ops, SparseCore 0:
  10.1 55.1 all-gather.5
  67.5 50.6 all-gather.7
  131.9 19.6 reduce-scatter.3
  153.0 21.2 all-gather.9
  176.3 37.8 all-gather.11
  216.3 20.4 all-reduce.5
  239.0 37.8 all-gather.13
  284.9 8.9 reduce-scatter.7
  296.1 20.3 reduce-scatter.5
  334.6 92.6 all-reduce.7
